TPU v7x, 32 devices: a whole 2x2x4 slice. The times are simulated.
32 devices in a mesh: wide: 8 (over y, x, core), narrow: 4 (over z).
Axes of the slice: x: 2, y: 2, z: 4, core: 2. Of those that a mesh axis runs over, the one named last changes fastest.
Arguments:
- node_features: bfloat16 [2048, 25, 128], P(('wide', 'narrow')), may hold values from -6 to 6
- frames: bfloat16 [2048, 48, 165], P(('wide', 'narrow')), may hold values from -6 to 6
- radial: bfloat16 [2048, 48, 128], P(('wide', 'narrow')), may hold values from 0.29882812 to 3
- neighbours: int32 [2048, 48], P(('wide', 'narrow')), may hold values from 0 to 2047, as said below
- counts: int32 [2048], P(('wide', 'narrow')), may hold values from 16 to 48
- coefficients: float32 [32], P('wide'), may hold values from 0.05 to 0.5
- w_zero: bfloat16 [32, 640, 640], P('wide'), may hold values from -0.25 to 0.25
- w_one: bfloat16 [32, 2, 512, 512], P('wide'), may hold values from -0.1875 to 0.1875
- w_two: bfloat16 [32, 2, 384, 384], P('wide'), may hold values from -0.21875 to 0.21875
- w_three: bfloat16 [32, 2, 256, 256], P('wide'), may hold values from -0.25 to 0.25
- w_four: bfloat16 [32, 2, 128, 128], P('wide'), may hold values from -0.375 to 0.375
Outputs:
- conv_out: float32 [2048, 25, 128], P(('wide', 'narrow'))
Inputs may be any that keep to these rules, and one draw needn't show every extreme that they name: `neighbours`: each neighbour of an atom lies in the atom's own aligned block of 64 atoms or in one of the two cyclically adjacent blocks. `counts`: slots at or beyond an atom's count are padding and carry arbitrary indices.
All inputs are finite; a program needn't handle non-finite values.
Results may differ from a plain program's by a relative error of at most 0.02.
Values may be sent and summed in bfloat16 or wider, within the bound.
A program may use at most 192 MiB of HBM per device.

v0:
```python
import jax
import jax.numpy as jnp
import numpy as np
from jax import lax
from jax.sharding import PartitionSpec as P


def extended_2(cells, sides, width):
    for axis, dim in sides:
        count = lax.axis_size(axis)
        head = lax.slice_in_dim(cells, 0, width, axis=dim)
        tail = lax.slice_in_dim(cells, cells.shape[dim] - width, cells.shape[dim], axis=dim)
        cells = jnp.concatenate(
            [
                lax.ppermute(tail, axis, [(i, (i + 1) % count) for i in range(count)]),
                cells,
                lax.ppermute(head, axis, [((i + 1) % count, i) for i in range(count)]),
            ],
            axis=dim,
        )
    return cells


def grouped_order():
    order_list = [degree * degree + degree for degree in range(5)]
    for order in range(1, 5):
        order_list += [degree * degree + degree + order for degree in range(order, 5)]
        order_list += [degree * degree + degree - order for degree in range(order, 5)]
    return order_list


def frame_table():
    position = np.zeros(25, np.int64)
    for place, component in enumerate(grouped_order()):
        position[component] = place
    table = np.zeros((165, 625), np.float32)
    offset = 0
    for degree in range(5):
        order_size = 2 * degree + 1
        for row in range(order_size):
            for column in range(order_size):
                target = position[degree * degree + row] * 25 + degree * degree + column
                table[offset + row * order_size + column, target] = 1.0
        offset += order_size * order_size
    return table


def block_weights(merged):
    result = [merged[0]]
    for order in range(1, 5):
        real_part = merged[order][0]
        imag_part = merged[order][1]
        upper = jnp.concatenate([real_part, imag_part], axis=1)
        lower = jnp.concatenate([-imag_part, real_part], axis=1)
        result.append(jnp.concatenate([upper, lower], axis=0))
    return result


def messages(gathered, frames, radial, weights, table):
    row_count = gathered.shape[0]
    channels = gathered.shape[2]
    dense = jnp.dot(frames, table, preferred_element_type=jnp.float32).reshape(row_count, 25, 25)
    dense_half = dense.astype(jnp.bfloat16)
    rotated = jnp.einsum("rpq,rqc->rpc", dense_half, gathered, preferred_element_type=jnp.float32)
    rotated = (rotated * radial.astype(jnp.float32)[:, None, :]).astype(jnp.bfloat16)
    pieces = []
    start = 0
    for order in range(5):
        width = 5 if order == 0 else 2 * (5 - order)
        inputs = rotated[:, start : start + width, :].reshape(row_count, width * channels)
        output = jnp.dot(inputs, weights[order], preferred_element_type=jnp.float32)
        pieces.append(output.reshape(row_count, width, channels))
        start += width
    mixed = jnp.concatenate(pieces, axis=1)
    scalar = mixed[:, 0:1, :]
    gated = jnp.concatenate([jax.nn.silu(scalar), mixed[:, 1:, :] * jax.nn.sigmoid(scalar)], axis=1)
    return jnp.einsum(
        "rqp,rqc->rpc",
        dense,
        gated,
        precision=lax.Precision.HIGHEST,
        preferred_element_type=jnp.float32,
    )


def body(
    node_features,
    frames,
    radial,
    neighbours,
    counts,
    coefficients,
    w_zero,
    w_one,
    w_two,
    w_three,
    w_four,
):
    atoms_here = node_features.shape[0]
    channels = node_features.shape[2]
    slot_total = neighbours.shape[1]
    extended = extended_2(node_features, ((("wide", "narrow"), 0),), atoms_here)
    experts_here = w_zero.shape[0]

    def combine(weights):
        summed_total = coefficients[0] * weights[0].astype(jnp.float32)
        for expert in range(1, experts_here):
            summed_total = summed_total + coefficients[expert] * weights[expert].astype(jnp.float32)
        return summed_total.astype(jnp.bfloat16)

    partial_zero = combine(w_zero)[None]
    partial_one = combine(w_one)
    partial_two = combine(w_two)
    partial_three = combine(w_three)
    partial_four = combine(w_four)
    shares = (
        lax.psum_scatter(partial_zero, "wide", scatter_dimension=1, tiled=True).astype(jnp.float32),
        lax.psum_scatter(partial_one, "wide", scatter_dimension=1, tiled=True).astype(jnp.float32),
        lax.psum_scatter(partial_two, "wide", scatter_dimension=1, tiled=True).astype(jnp.float32),
        lax.psum_scatter(partial_three, "wide", scatter_dimension=1, tiled=True).astype(
            jnp.float32
        ),
        lax.psum_scatter(partial_four, "wide", scatter_dimension=1, tiled=True).astype(jnp.float32),
    )
    merged_all = (
        lax.all_gather(shares[0].astype(jnp.bfloat16), "wide", axis=1, tiled=True),
        lax.all_gather(shares[1].astype(jnp.bfloat16), "wide", axis=1, tiled=True),
        lax.all_gather(shares[2].astype(jnp.bfloat16), "wide", axis=1, tiled=True),
        lax.all_gather(shares[3].astype(jnp.bfloat16), "wide", axis=1, tiled=True),
        lax.all_gather(shares[4].astype(jnp.bfloat16), "wide", axis=1, tiled=True),
    )
    merged = (merged_all[0][0], merged_all[1], merged_all[2], merged_all[3], merged_all[4])
    weights = block_weights(merged)
    table = jnp.asarray(frame_table()).astype(jnp.bfloat16)
    slot_group = 8
    for candidate in range(8, slot_total + 1, 8):
        if slot_total % candidate == 0 and atoms_here * candidate <= 1536:
            slot_group = candidate
    block_start = lax.axis_index(("wide", "narrow")) * atoms_here
    atoms_total = atoms_here * lax.axis_size(("wide", "narrow"))
    local_index = (neighbours - block_start + atoms_here) % atoms_total
    live_slots = (lax.broadcasted_iota(jnp.int32, neighbours.shape, 1) < counts[:, None]).astype(
        jnp.float32
    )

    def accumulate(carried, group_index):
        first_slot = group_index * slot_group
        index_block = lax.dynamic_slice_in_dim(local_index, first_slot, slot_group, 1).reshape(-1)
        frame_rows = lax.dynamic_slice_in_dim(frames, first_slot, slot_group, 1).reshape(
            -1, frames.shape[2]
        )
        radial_rows = lax.dynamic_slice_in_dim(radial, first_slot, slot_group, 1).reshape(
            -1, channels
        )
        live_block = lax.dynamic_slice_in_dim(live_slots, first_slot, slot_group, 1)
        gathered = jnp.take(extended, index_block, axis=0)
        result = messages(gathered, frame_rows, radial_rows, weights, table).reshape(
            atoms_here, slot_group, 25, channels
        )
        return (carried + jnp.sum(result * live_block[:, :, None, None], axis=1), None)

    initial = jnp.zeros((atoms_here, 25, channels), jnp.float32)
    summed_out, ignored = lax.scan(accumulate, initial, jnp.arange(slot_total // slot_group))
    return summed_out / jnp.sqrt(counts.astype(jnp.float32))[:, None, None]


def solution(mesh):
    in_specs = (
        P(("wide", "narrow"), None, None),
        P(("wide", "narrow"), None, None),
        P(("wide", "narrow"), None, None),
        P(("wide", "narrow"), None),
        P(("wide", "narrow")),
        P("wide"),
        P("wide", None, None),
        P("wide", None, None, None),
        P("wide", None, None, None),
        P("wide", None, None, None),
        P("wide", None, None, None),
    )
    out_specs = P(("wide", "narrow"), None, None)
    return jax.shard_map(body, mesh=mesh, in_specs=in_specs, out_specs=out_specs, check_vma=False)
```

profile of v0, /device:TPU:0, one launch (start us, length us, event | category | flops | bytes accessed | tf_op | source)
XLA Modules:
  0.0 558.8 jit_solution(3491979366544983716)
XLA Ops:
  8.0 5.6 fusion.13
  31.2 3.4 collective-permute-start.1
  34.5 3.4 fusion.24
  42.6 4.0 add_convert_fusion.1
  46.5 3.5 copy.255
  57.7 34.4 %all-reduce.7.cloned.1.call-done = (bf16[2,512,512]{2,0,1:T(2,128)(2,1)}, bf16[2,384,384]{2,0,1:T(2,128)(2,1)}, bf16[2,256,256]{2,0,1:T(2,128)(2,1)}, bf16[2,128,128]{2,0,1:T(2,128)(2,1)}) async-done(((bf16[2,512,512]{2,0,1:T(2,128)(2,1)}, bf16[2,384,384]{2,0,1:T(2,128)(2,1)}, bf16[2,256,256]{2,0,1:T(2,128)(2,1)}, bf16[2,128,128]{2,0,1:T(2,128)(2,1)}), (bf16[2,512,512]{2,0,1:T(2,128)(2,1)}, ...) | async-done | bytes 1966096
  93.0 8.9 %all_gather.17 = bf16[2,384,384]{2,0,1:T(2,128)(2,1)S(1)} all-gather(bf16[2,48,384]{2,0,1:T(2,128)(2,1)S(1)} %constant_dynamic-slice_fusion.6), channel_id=1, replica_groups=mesh['wide'=8,'narrow'=4] {'wide'}, dimensions={1}, use_global_device_ids=true | all-gather | bytes 663552 | tf_op jit(solution)/shard_map/all_gather | solution.py:128
  108.5 10.1 %all_gather.18 = bf16[2,256,256]{2,0,1:T(2,128)(2,1)S(1)} all-gather(bf16[2,32,256]{2,0,1:T(2,128)(2,1)S(1)} %constant_dynamic-slice_fusion.5), channel_id=1, replica_groups=mesh['wide'=8,'narrow'=4] {'wide'}, dimensions={1}, use_global_device_ids=true | all-gather | bytes 294912 | tf_op jit(solution)/shard_map/all_gather | solution.py:129
  120.7 8.4 %all_gather.19 = bf16[2,128,128]{2,0,1:T(2,128)(2,1)S(1)} all-gather(bf16[2,16,128]{2,0,1:T(2,128)(2,1)S(1)} %constant_dynamic-slice_fusion.4), channel_id=1, replica_groups=mesh['wide'=8,'narrow'=4] {'wide'}, dimensions={1}, use_global_device_ids=true | all-gather | bytes 73728 | tf_op jit(solution)/shard_map/all_gather | solution.py:130
  131.1 10.6 %all_gather.15 = bf16[1,640,640]{2,1,0:T(8,128)(2,1)S(1)} all-gather(bf16[1,80,640]{2,1,0:T(8,128)(2,1)S(1)} %copy.230), channel_id=1, replica_groups=mesh['wide'=8,'narrow'=4] {'wide'}, dimensions={1}, use_global_device_ids=true | all-gather | bytes 921600 | tf_op jit(solution)/shard_map/all_gather | solution.py:126
  143.0 11.2 %all-gather.2.cloned.1.call-done = bf16[2,512,512]{2,0,1:T(2,128)(2,1)} async-done(((bf16[2,64,512]{2,0,1:T(2,128)(2,1)}), bf16[2,512,512]{2,0,1:T(2,128)(2,1)}) %all-gather.2.cloned.1.call-update) | async-done | bytes 1048592 | tf_op jit(solution)/shard_map/all_gather | solution.py:127
  154.2 3.3 fusion.25
  159.4 4.0 copy.244
  163.4 385.9 %while.12 = (s32[]{:T(128)}, f32[64,25,128]{2,1,0:T(8,128)}, s32[2]{0:T(128)S(1)}, bf16[64,48,165]{2,1,0:T(8,128)(2,1)}, s32[64,48]{1,0:T(8,128)S(1)}, /*index=5...) while((s32[]{:T(128)}, f32[64,25,128]{2,1,0:T(8,128)}, ...), condition=%wide.region_7.8_spmd.clone.clone, body=%wide.region_5.7_spmd.clone.clone.sunk | while | flops 9371582464 | bytes 297412544 | solution.py:163
  183.3 3.8 fusion.79
  187.1 18.6 %copy.299 = bf16[1536,25,25]{2,1,0:T(8,128)(2,1)} copy(bf16[1536,25,25]{0,2,1:T(8,128)(2,1)} %get-tuple-element.430) | data formatting | bytes 3840000 | tf_op jit(solution)/shard_map/while/body/eval_jaxpr/convert_element_type | solution.py:63
  206.0 7.3 %gather_fusion = bf16[1536,25,128]{2,1,0:T(8,128)(2,1)} fusion(bf16[192,25,128]{2,1,0:T(8,128)(2,1)S(1)} %get-tuple-element.476, s32[2048]{0:T(1024)S(1)} %pad_clamp_fusion.2), kind=kCustom, calls=%fused_computation.clone.clone.clone.1 | custom fusion | bytes 19666944 | tf_op jit(solution)/shard_map/while/body/eval_jaxpr/jit(_take)/gather | solution.py:156
  214.5 15.9 %multiply_convert_fusion.2 = bf16[1536,25,128]{2,1,0:T(8,128)(2,1)} fusion(f32[1536,128]{1,0:T(8,128)S(1)} %bitcast_convert_fusion.2, bf16[1536,25,25]{2,1,0:T(8,128)(2,1)} %copy.299, bf16[1536,25,128]{2,1,0:T(8,128)(2,1)} %gather_fusion, pred[1536]{0:T(1024)(128)(4,1)S(1)} %compare_and_fusion.2), kind=kOutput, calls=%fused_computation.5.clone.1 | convolution fusion | flops 260505600 | bytes 22368768 | tf_op jit(solution)/shard_map/while/body/eval_jaxpr/rpq,rqc->rpc/dot_general | solution.py:64
  235.2 6.8 %constant_dynamic-update-slice_fusion.2 = (f32[1536,25,128]{2,0,1:T(8,128)}, f32[1536,5,128]{2,0,1:T(8,128)}) fusion(bf16[1536,640,1]{0,1,2:T(8,128)(2,1)} %bitcast.142, bf16[5,128,640]{2,1,0:T(8,128)(2,1)} %bitcast.145), kind=kOutput, calls=%fused_computation.23.clone.1 | convolution fusion | flops 1258291200 | bytes 10649600 | tf_op jit(solution)/shard_map/while/body/eval_jaxpr/dot_general | solution.py:71
  242.0 3.4 slice.247
  245.4 3.3 reshape.212
  248.7 7.4 %convolution_dynamic-update-slice_fusion.8 = f32[1536,25,128]{2,0,1:T(8,128)} fusion(f32[1536,25,128]{2,0,1:T(8,128)} %get-tuple-element.431, bf16[1536,1024,1]{1,0,2:T(8,128)(2,1)} %reshape.212, bf16[8,128,1024]{2,1,0:T(8,128)(2,1)} %bitcast.151), kind=kOutput, calls=%fused_computation.12.clone.1 | convolution fusion | flops 3221225472 | bytes 11534336 | tf_op jit(solution)/shard_map/while/body/eval_jaxpr/dot_general | solution.py:71
  256.1 3.4 slice.248
  262.5 6.3 %convolution_dynamic-update-slice_fusion.9 = f32[1536,25,128]{2,0,1:T(8,128)} fusion(f32[1536,25,128]{2,0,1:T(8,128)} %convolution_dynamic-update-slice_fusion.8, bf16[1536,768,1]{0,1,2:T(8,128)(2,1)} %bitcast.144, bf16[6,128,768]{2,1,0:T(8,128)(2,1)} %bitcast.152), kind=kOutput, calls=%fused_computation.13.clone.1 | convolution fusion | flops 1811939328 | bytes 8257536 | tf_op jit(solution)/shard_map/while/body/eval_jaxpr/dot_general | solution.py:71
  271.7 3.7 convolution_dynamic-update-slice_fusion.10
  275.5 3.4 slice.250
  282.3 7.1 %slice_multiply_fusion.5 = f32[1536,24,128]{2,0,1:T(8,128)S(1)} fusion(f32[1536,25,128]{2,0,1:T(8,128)} %convolution_dynamic-update-slice_fusion.11, f32[1536,128]{1,0:T(8,128)S(1)} %get-tuple-element.433), kind=kLoop, calls=%fused_computation.7.clone.1 | loop fusion | flops 4718592 | bytes 38535168 | tf_op jit(solution)/shard_map/while/body/eval_jaxpr/mul | solution.py:76
  289.4 7.0 %pad_maximum_fusion.3 = f32[1536,25,128]{2,0,1:T(8,128)} fusion(f32[1536,24,128]{2,0,1:T(8,128)S(1)} %slice_multiply_fusion.5, f32[1536,1,128]{2,0,1:T(8,128)S(1)} %get-tuple-element.434), kind=kLoop, calls=%fused_computation.6.clone.1 | loop fusion | flops 4915200 | bytes 39321600 | tf_op jit(solution)/shard_map/while/body/eval_jaxpr/concatenate | solution.py:76
  296.4 20.9 %copy.298 = f32[1536,25,25]{1,2,0:T(8,128)} copy(f32[1536,25,25]{0,2,1:T(8,128)} %get-tuple-element.429) | data formatting | bytes 7680000 | tf_op jit(solution)/shard_map/while/body/eval_jaxpr/dot_general | solution.py:62
  317.3 40.7 %fusion.81 = f32[1536,25,128]{2,1,0:T(8,128)S(1)} fusion(f32[1536,25,25]{1,2,0:T(8,128)} %copy.298, f32[1536,25,128]{2,0,1:T(8,128)} %pad_maximum_fusion.3), kind=kOutput, calls=%fused_computation.2.clone.1 | convolution fusion | flops 1474560000 | bytes 43161600 | tf_op jit(solution)/shard_map/while/body/eval_jaxpr/rqp,rqc->rpc/dot_general | solution.py:77
  358.1 4.2 multiply_reduce_fusion.2
  367.5 3.8 fusion.79
  371.3 18.6 %copy.299 = bf16[1536,25,25]{2,1,0:T(8,128)(2,1)} copy(bf16[1536,25,25]{0,2,1:T(8,128)(2,1)} %get-tuple-element.430) | data formatting | bytes 3840000 | tf_op jit(solution)/shard_map/while/body/eval_jaxpr/convert_element_type | solution.py:63
  390.1 7.3 %gather_fusion = bf16[1536,25,128]{2,1,0:T(8,128)(2,1)} fusion(bf16[192,25,128]{2,1,0:T(8,128)(2,1)S(1)} %get-tuple-element.476, s32[2048]{0:T(1024)S(1)} %pad_clamp_fusion.2), kind=kCustom, calls=%fused_computation.clone.clone.clone.1 | custom fusion | bytes 19666944 | tf_op jit(solution)/shard_map/while/body/eval_jaxpr/jit(_take)/gather | solution.py:156
  398.7 15.9 %multiply_convert_fusion.2 = bf16[1536,25,128]{2,1,0:T(8,128)(2,1)} fusion(f32[1536,128]{1,0:T(8,128)S(1)} %bitcast_convert_fusion.2, bf16[1536,25,25]{2,1,0:T(8,128)(2,1)} %copy.299, bf16[1536,25,128]{2,1,0:T(8,128)(2,1)} %gather_fusion, pred[1536]{0:T(1024)(128)(4,1)S(1)} %compare_and_fusion.2), kind=kOutput, calls=%fused_computation.5.clone.1 | convolution fusion | flops 260505600 | bytes 22368768 | tf_op jit(solution)/shard_map/while/body/eval_jaxpr/rpq,rqc->rpc/dot_general | solution.py:64
  419.4 6.8 %constant_dynamic-update-slice_fusion.2 = (f32[1536,25,128]{2,0,1:T(8,128)}, f32[1536,5,128]{2,0,1:T(8,128)}) fusion(bf16[1536,640,1]{0,1,2:T(8,128)(2,1)} %bitcast.142, bf16[5,128,640]{2,1,0:T(8,128)(2,1)} %bitcast.145), kind=kOutput, calls=%fused_computation.23.clone.1 | convolution fusion | flops 1258291200 | bytes 10649600 | tf_op jit(solution)/shard_map/while/body/eval_jaxpr/dot_general | solution.py:71
  426.2 3.4 slice.247
  429.6 3.3 reshape.212
  432.9 7.4 %convolution_dynamic-update-slice_fusion.8 = f32[1536,25,128]{2,0,1:T(8,128)} fusion(f32[1536,25,128]{2,0,1:T(8,128)} %get-tuple-element.431, bf16[1536,1024,1]{1,0,2:T(8,128)(2,1)} %reshape.212, bf16[8,128,1024]{2,1,0:T(8,128)(2,1)} %bitcast.151), kind=kOutput, calls=%fused_computation.12.clone.1 | convolution fusion | flops 3221225472 | bytes 11534336 | tf_op jit(solution)/shard_map/while/body/eval_jaxpr/dot_general | solution.py:71
  440.3 3.4 slice.248
  446.7 6.3 %convolution_dynamic-update-slice_fusion.9 = f32[1536,25,128]{2,0,1:T(8,128)} fusion(f32[1536,25,128]{2,0,1:T(8,128)} %convolution_dynamic-update-slice_fusion.8, bf16[1536,768,1]{0,1,2:T(8,128)(2,1)} %bitcast.144, bf16[6,128,768]{2,1,0:T(8,128)(2,1)} %bitcast.152), kind=kOutput, calls=%fused_computation.13.clone.1 | convolution fusion | flops 1811939328 | bytes 8257536 | tf_op jit(solution)/shard_map/while/body/eval_jaxpr/dot_general | solution.py:71
  455.9 3.7 convolution_dynamic-update-slice_fusion.10
  459.7 3.4 slice.250
  466.5 7.1 %slice_multiply_fusion.5 = f32[1536,24,128]{2,0,1:T(8,128)S(1)} fusion(f32[1536,25,128]{2,0,1:T(8,128)} %convolution_dynamic-update-slice_fusion.11, f32[1536,128]{1,0:T(8,128)S(1)} %get-tuple-element.433), kind=kLoop, calls=%fused_computation.7.clone.1 | loop fusion | flops 4718592 | bytes 38535168 | tf_op jit(solution)/shard_map/while/body/eval_jaxpr/mul | solution.py:76
  473.6 7.0 %pad_maximum_fusion.3 = f32[1536,25,128]{2,0,1:T(8,128)} fusion(f32[1536,24,128]{2,0,1:T(8,128)S(1)} %slice_multiply_fusion.5, f32[1536,1,128]{2,0,1:T(8,128)S(1)} %get-tuple-element.434), kind=kLoop, calls=%fused_computation.6.clone.1 | loop fusion | flops 4915200 | bytes 39321600 | tf_op jit(solution)/shard_map/while/body/eval_jaxpr/concatenate | solution.py:76
  480.6 20.9 %copy.298 = f32[1536,25,25]{1,2,0:T(8,128)} copy(f32[1536,25,25]{0,2,1:T(8,128)} %get-tuple-element.429) | data formatting | bytes 7680000 | tf_op jit(solution)/shard_map/while/body/eval_jaxpr/dot_general | solution.py:62
  501.5 40.7 %fusion.81 = f32[1536,25,128]{2,1,0:T(8,128)S(1)} fusion(f32[1536,25,25]{1,2,0:T(8,128)} %copy.298, f32[1536,25,128]{2,0,1:T(8,128)} %pad_maximum_fusion.3), kind=kOutput, calls=%fused_computation.2.clone.1 | convolution fusion | flops 1474560000 | bytes 43161600 | tf_op jit(solution)/shard_map/while/body/eval_jaxpr/rqp,rqc->rpc/dot_general | solution.py:77
  542.3 4.2 multiply_reduce_fusion.2
  (146 shorter events, 87.0 us)
Async XLA Ops:
  6.5 85.5 %all-reduce.7.cloned.1.call-start = ((), (), s32[]{:S(2)}) async-start(), calls=%async_computation.3 | async-start | bytes 3932160
  8.0 7.6 %copy-start.4 = (bf16[4,2,384,384]{3,2,1,0:T(8,128)(2,1)S(1)}, bf16[4,2,384,384]{3,2,1,0:T(8,128)(2,1)}, u32[]{:S(2)}) copy-start(bf16[4,2,384,384]{3,2,1,0:T(8,128)(2,1)} %param.22) | copy-start | bytes 7077892
  15.6 4.4 copy-start.8
  15.6 8.1 %copy-start.10 = (bf16[4,2,128,128]{3,2,1,0:T(8,128)(2,1)S(1)}, bf16[4,2,128,128]{3,2,1,0:T(8,128)(2,1)}, u32[]{:S(2)}) copy-start(bf16[4,2,128,128]{3,2,1,0:T(8,128)(2,1)} %param.24) | copy-start | bytes 786436
  20.0 7.0 %copy-start.9 = (bf16[64,25,128]{2,0,1:T(8,128)(2,1)S(1)}, bf16[64,25,128]{2,0,1:T(8,128)(2,1)}, u32[]{:S(2)}) copy-start(bf16[64,25,128]{2,0,1:T(8,128)(2,1)} %param.14) | copy-start | bytes 1228804
  27.0 103.1 %reduce-scatter.4.cloned.1.call-start = ((), (), s32[]{:S(2)}) async-start(), calls=%async_computation.2 | async-start | bytes 921600
  28.1 27.4 %collective-permute-start = (bf16[64,25,128]{2,1,0:T(8,128)(2,1)}, bf16[64,25,128]{2,1,0:T(8,128)(2,1)}, u32[]{:S(2)}, u32[]{:S(2)}) collective-permute-start(bf16[64,25,128]{2,1,0:T(8,128)(2,1)} %copy.223), channel_id=1, source_target_pairs={{0,1},{1,2},{2,3},{3,4},{4,5},{5,6},{6,7},{7,8},{8,9},{9,10},{10,1... | collective-permute-start | bytes 1228808 | tf_op jit(solution)/shard_map/ppermute | solution.py:15
  31.2 24.9 %collective-permute-start.1 = (bf16[64,25,128]{2,1,0:T(8,128)(2,1)}, bf16[64,25,128]{2,1,0:T(8,128)(2,1)}, u32[]{:S(2)}, u32[]{:S(2)}) collective-permute-start(bf16[64,25,128]{2,1,0:T(8,128)(2,1)} %copy.223), channel_id=1, source_target_pairs={{1,0},{2,1},{3,2},{4,3},{5,4},{6,5},{7,6},{8,7},{9,8},{10,9},{11,1... | collective-permute-start | bytes 1228808 | tf_op jit(solution)/shard_map/ppermute | solution.py:17
  46.5 4.7 copy-start.15
  46.5 7.5 %copy-start.11 = (s32[64,48]{0,1:T(8,128)S(1)}, s32[64,48]{0,1:T(8,128)}, u32[]{:S(2)}) copy-start(s32[64,48]{0,1:T(8,128)} %param.17) | copy-start | bytes 36868
  46.5 7.7 %copy-start.12 = (s32[64]{0:T(128)S(1)}, s32[64]{0:T(128)}, u32[]{:S(2)}) copy-start(s32[64]{0:T(128)} %param.18) | copy-start | bytes 772
  51.1 103.1 %all-gather.2.cloned.1.call-start = ((), (), s32[]{:S(2)}) async-start(), calls=%async_computation.1 | async-start | bytes 1179648 | tf_op jit(solution)/shard_map/all_gather | solution.py:127
  159.4 4.0 copy-start.2
  180.6 6.5 %copy-start.13 = (s32[2]{0:T(128)}, s32[2]{0:T(128)S(1)}, u32[]{:S(2)}) copy-start(s32[2]{0:T(128)S(1)} %get-tuple-element.473) | copy-start | bytes 28 | tf_op jit(solution)/shard_map/while
  180.6 25.1 %copy-start.5 = (s32[64,48]{1,0:T(8,128)}, s32[64,48]{1,0:T(8,128)S(1)}, u32[]{:S(2)}) copy-start(s32[64,48]{1,0:T(8,128)S(1)} %get-tuple-element.475) | copy-start | bytes 36868 | tf_op jit(solution)/shard_map/while
  180.7 25.3 %copy-start = (bf16[192,25,128]{2,1,0:T(8,128)(2,1)}, bf16[192,25,128]{2,1,0:T(8,128)(2,1)S(1)}, u32[]{:S(2)}) copy-start(bf16[192,25,128]{2,1,0:T(8,128)(2,1)S(1)} %get-tuple-element.476) | copy-start | bytes 3686404 | tf_op jit(solution)/shard_map/while
  275.5 3.9 copy-start.3
  317.3 40.7 %copy-start.7 = (f32[64,48]{1,0:T(8,128)S(1)}, f32[64,48]{1,0:T(8,128)}, u32[]{:S(2)}) copy-start(f32[64,48]{1,0:T(8,128)} %get-tuple-element.483) | copy-start | bytes 36868 | tf_op jit(solution)/shard_map/while
  362.2 2.6 copy-start.1
  362.2 2.6 copy-start.6
  362.2 2.6 copy-start.14
  364.8 6.5 %copy-start.13 = (s32[2]{0:T(128)}, s32[2]{0:T(128)S(1)}, u32[]{:S(2)}) copy-start(s32[2]{0:T(128)S(1)} %get-tuple-element.473) | copy-start | bytes 28 | tf_op jit(solution)/shard_map/while
  364.8 25.1 %copy-start.5 = (s32[64,48]{1,0:T(8,128)}, s32[64,48]{1,0:T(8,128)S(1)}, u32[]{:S(2)}) copy-start(s32[64,48]{1,0:T(8,128)S(1)} %get-tuple-element.475) | copy-start | bytes 36868 | tf_op jit(solution)/shard_map/while
  364.8 25.3 %copy-start = (bf16[192,25,128]{2,1,0:T(8,128)(2,1)}, bf16[192,25,128]{2,1,0:T(8,128)(2,1)S(1)}, u32[]{:S(2)}) copy-start(bf16[192,25,128]{2,1,0:T(8,128)(2,1)S(1)} %get-tuple-element.476) | copy-start | bytes 3686404 | tf_op jit(solution)/shard_map/while
  459.7 3.9 copy-start.3
  501.5 40.7 %copy-start.7 = (f32[64,48]{1,0:T(8,128)S(1)}, f32[64,48]{1,0:T(8,128)}, u32[]{:S(2)}) copy-start(f32[64,48]{1,0:T(8,128)} %get-tuple-element.483) | copy-start | bytes 36868 | tf_op jit(solution)/shard_map/while
  546.4 2.9 copy-start.1
  546.4 2.9 copy-start.6
  546.4 2.9 copy-start.14
Sparse Core Ops, SparseCore 0:
  27.1 64.8 all-reduce.6
  95.4 33.4 reduce-scatter.3
  130.8 23.3 all-gather.1
where the time goes:
time: 569 us; the launch traced here: 559 us
  local copies, waits for them, and re-layouts  189 us (33%)
  matrix products  172 us (30%)
  other arithmetic  71.9 us (13%)
  waiting for transfers between devices  46.3 us (8%)
  blocking collectives  37.9 us (7%)
  loops' own time  19 us (3%)
  between operations  16 us (3%)
  starting transfers between devices  6.49 us (1%)
    dot_general x2, matrix products, messages(): jnp.einsum('rqp,rqc->rpc', dense, gated, precision=lax.Precision.HIGHEST,...  81.3 us
    dot_general x10, matrix products, messages(): output = jnp.dot(inputs, weights[order], preferred_element_type=jnp.float32)  51.4 us
    dot_general x2, local copies, waits for them, and re-layouts, messages(): jnp.dot(frames, table, preferred_element_type=jnp.float32)  41.8 us
    slice x14, local copies, waits for them, and re-layouts, messages(): rotated[:, start:start + width, :].reshape(row_count, width * channels)  40.6 us
    convert_element_type x2, local copies, waits for them, and re-layouts, messages(): dense_half = dense.astype(jnp.bfloat16)  37.2 us
    unnamed x5, waiting for transfers between devices  34.4 us
    dot_general x2, matrix products, messages(): jnp.einsum('rpq,rqc->rpc', dense_half, gathered, preferred_element_type=j...  31.7 us
    unnamed x39, local copies, waits for them, and re-layouts  24.7 us
  transfers between devices with their start and end apart: 5, of which 3 were waited for; matrix products, arithmetic and copies ran while one was open for 6% of the time, Pallas kernels for 0%

commit v1 on v0

v1 whole, which is shorter than its diff:
```python
import functools

import jax
import jax.numpy as jnp
import numpy as np
from jax import lax
from jax.experimental import pallas as pl
from jax.experimental.pallas import tpu as pltpu
from jax.sharding import PartitionSpec as P

DEGREES = 5
COMPONENTS = DEGREES * DEGREES
AXES = ("wide", "narrow")


def halo(cells):
    count = lax.axis_size(AXES)
    below = lax.ppermute(cells, AXES, [(i, (i + 1) % count) for i in range(count)])
    above = lax.ppermute(cells, AXES, [((i + 1) % count, i) for i in range(count)])
    return jnp.concatenate([below, cells, above], axis=0)


def flat_rows(weights):
    return weights.reshape(weights.shape[0], -1, weights.shape[-1])


def merge_weights(coefficients, stacks):
    members = lax.axis_size("narrow")
    member = lax.axis_index("narrow")
    pieces = []
    for weights in stacks:
        weights = flat_rows(weights)
        rows = weights.shape[1] // members
        mine = lax.dynamic_slice_in_dim(weights, member * rows, rows, 1)
        total = coefficients[0] * mine[0].astype(jnp.float32)
        for expert in range(1, weights.shape[0]):
            total = total + coefficients[expert] * mine[expert].astype(jnp.float32)
        total = total.astype(jnp.bfloat16)
        for block in range(total.shape[1] // 128):
            pieces.append(total[:, block * 128 : (block + 1) * 128])
    rows = sum(piece.shape[0] for piece in pieces)
    unit = 16 * lax.axis_size("wide")
    pieces.append(jnp.zeros((-rows % unit, 128), jnp.bfloat16))
    partial = jnp.concatenate(pieces, axis=0)
    share = lax.psum_scatter(partial, "wide", scatter_dimension=0, tiled=True)
    gathered = lax.all_gather(share, ("narrow", "wide"), axis=0, tiled=True)
    return gathered.reshape(members, -1, 128)


def conv_kernel(
    shapes,
    index_ref,
    live_ref,
    frames_ref,
    radial_ref,
    features_ref,
    merged_ref,
    scale_ref,
    out_ref,
    source_ref,
    turned_ref,
    gated_ref,
    frame_ref,
    total_ref,
    *weight_refs,
):
    step = pl.program_id(0)
    channels = radial_ref.shape[0]
    lanes = index_ref.shape[1]
    atoms = out_ref.shape[0]
    extended = features_ref.shape[1]
    members = merged_ref.shape[0]

    @pl.when(step == 0)
    def _():
        total_ref[...] = jnp.zeros_like(total_ref)
        offset = 0
        for weight_ref, (rows, columns) in zip(weight_refs, shapes):
            part = rows // members
            for block in range(columns // 128):
                whole = jnp.concatenate(
                    [merged_ref[m, pl.ds(offset, part), :] for m in range(members)], axis=0
                )
                weight_ref[pl.ds(block * 128, 128), :] = jnp.transpose(whole)
                offset += part

    for k in range(frames_ref.shape[0]):
        row = frames_ref[pl.ds(k, 1), :]
        frame_ref[k] = jnp.broadcast_to(row, (16, lanes)).astype(jnp.bfloat16)

    picked = (
        lax.broadcasted_iota(jnp.int32, (extended, lanes), 0) == index_ref[...]
    ).astype(jnp.bfloat16)

    for component in range(COMPONENTS):
        block = pl.ds(component * channels, channels)
        source_ref[block, :] = jnp.dot(
            features_ref[block, :], picked, preferred_element_type=jnp.float32
        ).astype(jnp.bfloat16)

    starts = []
    start = 0
    for order in range(DEGREES):
        starts.append(start)
        start += (DEGREES - order) * (1 if order == 0 else 2)

    row_tiles = channels // 16
    lane_tiles = lanes // 128

    def rotate(i, carried):
        row = pl.multiple_of((i // lane_tiles) * 16, 16)
        lane = pl.ds(pl.multiple_of((i % lane_tiles) * 128, 128), 128)
        radial = radial_ref[pl.ds(row, 16), lane]
        offset = 0
        for degree in range(DEGREES):
            size = 2 * degree + 1
            xs = [
                source_ref[
                    pl.ds(pl.multiple_of((degree * degree + q) * channels + row, 16), 16), lane
                ]
                for q in range(size)
            ]
            for p in range(size):
                value = frame_ref[offset + p * size, :, lane] * xs[0]
                for q in range(1, size):
                    value = value + frame_ref[offset + p * size + q, :, lane] * xs[q]
                value = value * radial
                order = abs(p - degree)
                kept = DEGREES - order
                place = starts[order] + degree - order
                if order == 0:
                    turned_ref[0, pl.ds(pl.multiple_of(place * channels + row, 16), 16), lane] = value
                else:
                    upper = pl.ds(pl.multiple_of(place * channels + row, 16), 16)
                    lower = pl.ds(pl.multiple_of((place + kept) * channels + row, 16), 16)
                    if p > degree:
                        turned_ref[0, upper, lane] = value
                        turned_ref[1, lower, lane] = value
                    else:
                        turned_ref[0, lower, lane] = -value
                        turned_ref[1, upper, lane] = value
            offset += size * size
        return carried

    lax.fori_loop(0, row_tiles * lane_tiles, rotate, 0)

    central = jnp.dot(
        weight_refs[0][...],
        turned_ref[0, pl.ds(0, DEGREES * channels), :],
        preferred_element_type=jnp.float32,
    )
    scalar = central[:channels]
    gate = live_ref[...] / (1.0 + jnp.exp(-scalar))
    for degree in range(DEGREES):
        gated_ref[pl.ds((degree * degree + degree) * channels, channels), :] = (
            central[degree * channels : (degree + 1) * channels] * gate
        ).astype(jnp.bfloat16)
    for order in range(1, DEGREES):
        kept = DEGREES - order
        span = pl.ds(starts[order] * channels, 2 * kept * channels)
        for side in range(2):
            mixed = jnp.dot(
                weight_refs[order][...],
                turned_ref[side, span, :],
                preferred_element_type=jnp.float32,
            )
            for column in range(kept):
                degree = order + column
                component = degree * degree + degree + (order if side == 0 else -order)
                gated_ref[pl.ds(component * channels, channels), :] = (
                    mixed[column * channels : (column + 1) * channels] * gate
                ).astype(jnp.bfloat16)

    def unrotate(i, carried):
        row = pl.multiple_of(i * 16, 16)
        offset = 0
        for degree in range(DEGREES):
            size = 2 * degree + 1
            sums = [None] * size
            for tile in range(lane_tiles):
                lane = pl.ds(tile * 128, 128)
                ys = [
                    gated_ref[
                        pl.ds(pl.multiple_of((degree * degree + q) * channels + row, 16), 16), lane
                    ]
                    for q in range(size)
                ]
                for p in range(size):
                    value = frame_ref[offset + p, :, lane] * ys[0]
                    for q in range(1, size):
                        value = value + frame_ref[offset + q * size + p, :, lane] * ys[q]
                    value = value.astype(jnp.float32)
                    sums[p] = value if sums[p] is None else sums[p] + value
            for p in range(size):
                place = pl.ds(pl.multiple_of((degree * degree + p) * channels + row, 16), 16)
                total_ref[place, :] = total_ref[place, :] + sums[p]
            offset += size * size
        return carried

    lax.fori_loop(0, row_tiles, unrotate, 0)

    @pl.when(step == pl.num_programs(0) - 1)
    def _():
        for component in range(COMPONENTS):
            block = jnp.transpose(total_ref[pl.ds(component * channels, channels), :])
            total = block[:atoms]
            for part in range(1, 128 // atoms):
                total = total + block[part * atoms : (part + 1) * atoms]
            out_ref[:, component, :] = total * scale_ref[...]


def body(
    node_features,
    frames,
    radial,
    neighbours,
    counts,
    coefficients,
    w_zero,
    w_one,
    w_two,
    w_three,
    w_four,
):
    atoms, components, channels = node_features.shape
    slots = neighbours.shape[1]
    entries = frames.shape[2]
    edges = atoms * slots
    stacks = (w_zero, w_one, w_two, w_three, w_four)
    merged = merge_weights(coefficients, stacks)
    shapes = [(int(np.prod(w.shape[1:-1])), w.shape[-1]) for w in stacks]

    features = halo(node_features).reshape(3 * atoms, components * channels).T
    block_start = lax.axis_index(AXES) * atoms
    atoms_total = atoms * lax.axis_size(AXES)
    index = ((neighbours - block_start + atoms) % atoms_total).T.reshape(1, edges)
    live = (lax.broadcasted_iota(jnp.int32, (slots, atoms), 0) < counts[None, :]).astype(
        jnp.float32
    ).reshape(1, edges)
    frames_t = frames.transpose(2, 1, 0).reshape(entries, edges).astype(jnp.float32)
    radial_t = radial.transpose(2, 1, 0).reshape(channels, edges)
    scale = jnp.broadcast_to(
        (1.0 / jnp.sqrt(counts.astype(jnp.float32)))[:, None], (atoms, channels)
    )

    lanes = 256
    whole = lambda shape: pl.BlockSpec(shape, lambda i: (0,) * len(shape))
    columns = lambda rows: pl.BlockSpec((rows, lanes), lambda i: (0, i))
    return pl.pallas_call(
        functools.partial(conv_kernel, shapes),
        grid=(edges // lanes,),
        in_specs=[
            columns(1),
            columns(1),
            columns(entries),
            columns(channels),
            whole(features.shape),
            whole(merged.shape),
            whole(scale.shape),
        ],
        out_specs=whole((atoms, components, channels)),
        out_shape=jax.ShapeDtypeStruct((atoms, components, channels), jnp.float32),
        scratch_shapes=[
            pltpu.VMEM((components * channels, lanes), jnp.bfloat16),
            pltpu.VMEM((2, (2 * components - DEGREES) * channels, lanes), jnp.bfloat16),
            pltpu.VMEM((components * channels, lanes), jnp.bfloat16),
            pltpu.VMEM((entries, 16, lanes), jnp.bfloat16),
            pltpu.VMEM((components * channels, 128), jnp.float32),
        ]
        + [pltpu.VMEM((n, k), jnp.bfloat16) for k, n in shapes],
        compiler_params=pltpu.CompilerParams(
            dimension_semantics=("arbitrary",), vmem_limit_bytes=56 * 1024 * 1024
        ),
    )(index, live, frames_t, radial_t, features, merged, scale)


def solution(mesh):
    spread = lambda rest: P(AXES, *([None] * rest))
    in_specs = (
        spread(2),
        spread(2),
        spread(2),
        spread(1),
        spread(0),
        P("wide"),
        P("wide", None, None),
        P("wide", None, None, None),
        P("wide", None, None, None),
        P("wide", None, None, None),
        P("wide", None, None, None),
    )
    return jax.shard_map(body, mesh=mesh, in_specs=in_specs, out_specs=spread(2), check_vma=False)
```

time: 569 us -> 215 us (0.38); the launches traced: 559 us -> 215 us
  local copies, waits for them, and re-layouts: 189 us -> 15.9 us
  matrix products: 172 us -> 0 us
  Pallas kernels: 0 us -> 76.2 us
  other arithmetic: 71.9 us -> 20 us
  waiting for transfers between devices: 46.3 us -> 86 us
  blocking collectives: 37.9 us -> 0 us
  loops' own time: 19 us -> 0 us
    dot_general x16 -> x0, matrix products: 172 us -> none  [the longest x2 81.3 us: messages(): jnp.einsum('rqp,rqc->rpc', dense, gated, precision=lax.Precision.HIGHEST,...]
    pallas_call x0 -> x1, Pallas kernels: none -> 76.2 us  [body(): pl.pallas_call(functools.partial(conv_kernel, shapes), grid=(edges // lan...]
    slice x20 -> x1, local copies, waits for them, and re-layouts: 50 us -> 1.42 us  [merge_weights(): total = coefficients[0] * mine[0].astype(jnp.float32)]
    dot_general x2 -> x0, local copies, waits for them, and re-layouts: 41.8 us -> none  [messages(): jnp.dot(frames, table, preferred_element_type=jnp.float32)]
    all_gather x4 -> x0, blocking collectives: 37.9 us -> none  [the longest x1 10.6 us: body(): lax.all_gather(shares[0].astype(jnp.bfloat16), 'wide', axis=1, tiled=True)]
    convert_element_type x6 -> x3, local copies, waits for them, and re-layouts: 42.3 us -> 4.65 us  [the longest x2 3.98 us: body(): frames.transpose(2, 1, 0).reshape(entries, edges).astype(jnp.float32)]
    reduce_scatter x0 -> x1, waiting for transfers between devices: none -> 37.6 us  [merge_weights(): share = lax.psum_scatter(partial, 'wide', scatter_dimension=0, tiled=True)]
    unnamed x5 -> x2, waiting for transfers between devices: 34.4 us -> 0.03 us
  transfers between devices with their start and end apart: 5 -> 4, of which waited for: 3 -> 4; matrix products, arithmetic and copies ran while one was open for 6% -> 5% of each run, Pallas kernels for 0% -> 0%
where the time goes in v1:
time: 215 us
  waiting for transfers between devices  86 us (40%)
  Pallas kernels  76.2 us (35%)
  other arithmetic  20 us (9%)
  local copies, waits for them, and re-layouts  15.9 us (7%)
  between operations  13.6 us (6%)
  starting transfers between devices  3.2 us (1%)
    pallas_call x1, Pallas kernels, body(): pl.pallas_call(functools.partial(conv_kernel, shapes), grid=(edges // lan...  76.2 us
    reduce_scatter x1, waiting for transfers between devices, merge_weights(): share = lax.psum_scatter(partial, 'wide', scatter_dimension=0, tiled=True)  37.6 us
    all_gather x1, waiting for transfers between devices, merge_weights(): gathered = lax.all_gather(share, ('narrow', 'wide'), axis=0, tiled=True)  36.4 us
    convert_element_type x4, other arithmetic, merge_weights(): total = total.astype(jnp.bfloat16)  15 us
    ppermute x1, waiting for transfers between devices, halo(): lax.ppermute(cells, AXES, [(i, (i + 1) % count) for i in range(count)])  9.7 us
  transfers between devices with their start and end apart: 4, of which 4 were waited for; matrix products, arithmetic and copies ran while one was open for 5% of the time, Pallas kernels for 0%

profile of v1, /device:TPU:0, one launch (start us, length us, event | category | flops | bytes accessed | tf_op | source)
XLA Modules:
  0.0 214.8 jit_solution(509220416187595261)
XLA Ops:
  6.5 0.0 reduce-scatter.2.cloned.1.call-start
  6.5 1.4 fusion.8
  8.0 3.9 %fusion.1 = bf16[160,640]{1,0:T(8,128)(2,1)S(1)} fusion(bf16[4,640,640]{2,1,0:T(8,128)(2,1)} %param.17, s32[]{:T(128)S(6)} %add.133, s32[]{:T(128)S(6)} %select_n.23, s32[]{:T(128)S(6)} %add.132, s32[]{:T(128)S(6)} %add.131, f32[]{:T(128)} %bitcast.10, f32[]{:T(128)} %bitcast.9, f32[]{:T(128)} %bitcast.8, f32[]{:T(128)} %bitcast.7), kind=kLoop, calls=%fused_computation.6 | loop fusion | flops 1228800 | bytes 1024032 | tf_op jit(solution)/shard_map/convert_element_type | solution.py:38
  11.8 0.0 copy-start.2
  11.8 0.0 copy-start.3
  11.9 0.0 copy-start.4
  11.9 0.0 copy-start
  12.0 4.0 %fusion = bf16[256,512]{1,0:T(8,128)(2,1)S(1)} fusion(bf16[4,1024,512]{2,1,0:T(8,128)(2,1)} %bitcast.36, s32[]{:T(128)S(6)} %add.133, s32[]{:T(128)S(6)} %select_n.24, s32[]{:T(128)S(6)} %add.132, s32[]{:T(128)S(6)} %add.131, f32[]{:T(128)} %bitcast.10, f32[]{:T(128)} %bitcast.9, f32[]{:T(128)} %bitcast.8, f32[]{:T(128)} %bitcast.7), kind=kLoop, calls=%fused_computation.5 | loop fusion | flops 1572864 | bytes 1310752 | tf_op jit(solution)/shard_map/convert_element_type | solution.py:38
  16.0 3.7 %fusion.2 = bf16[192,384]{1,0:T(8,128)(2,1)S(1)} fusion(bf16[4,768,384]{2,1,0:T(8,128)(2,1)} %bitcast.37, s32[]{:T(128)S(6)} %add.133, s32[]{:T(128)S(6)} %select_n.25, s32[]{:T(128)S(6)} %add.132, s32[]{:T(128)S(6)} %add.131, f32[]{:T(128)} %bitcast.10, f32[]{:T(128)} %bitcast.9, f32[]{:T(128)} %bitcast.8, f32[]{:T(128)} %bitcast.7), kind=kLoop, calls=%fused_computation.7 | loop fusion | flops 884736 | bytes 737312 | tf_op jit(solution)/shard_map/convert_element_type | solution.py:38
  19.8 3.5 %fusion.3 = bf16[128,256]{1,0:T(8,128)(2,1)S(1)} fusion(bf16[4,512,256]{2,1,0:T(8,128)(2,1)} %bitcast.38, s32[]{:T(128)S(6)} %add.133, s32[]{:T(128)S(6)} %select_n.26, s32[]{:T(128)S(6)} %add.132, s32[]{:T(128)S(6)} %add.131, f32[]{:T(128)} %bitcast.10, f32[]{:T(128)} %bitcast.9, f32[]{:T(128)} %bitcast.8, f32[]{:T(128)} %bitcast.7), kind=kLoop, calls=%fused_computation.9 | loop fusion | flops 393216 | bytes 327712 | tf_op jit(solution)/shard_map/convert_element_type | solution.py:38
  23.3 3.3 %constant_dynamic-update-slice_fusion.1 = bf16[2816,128]{1,0:T(8,128)(2,1)S(1)} fusion(bf16[2816,128]{1,0:T(8,128)(2,1)S(1)} %constant_dynamic-update-slice_fusion.2, bf16[4,256,128]{2,1,0:T(8,128)(2,1)} %bitcast.39, s32[]{:T(128)S(6)} %add.133, s32[]{:T(128)S(6)} %select_n.27, s32[]{:T(128)S(6)} %add.132, s32[]{:T(128)S(6)} %add.131, f32[]{:T(128)} %bitcast.10, ...), kind=kLoop, calls=%fused_computation.26 | loop fusion | flops 98304 | bytes 81952
  26.6 0.0 copy-start.1
  26.6 0.8 copy-done.1
  27.5 0.0 reduce-scatter.2.cloned.1.call-update
  27.5 0.0 all-gather.2.cloned.1.call-start
  27.5 37.6 %reduce-scatter.2.cloned.1.call-done = bf16[352,128]{1,0:T(8,128)(2,1)} async-done(((bf16[2816,128]{1,0:T(8,128)(2,1)}), bf16[352,128]{1,0:T(8,128)(2,1)}) %reduce-scatter.2.cloned.1.call-update) | async-done | bytes 90128 | tf_op jit(solution)/shard_map/reduce_scatter | solution.py:45
  65.1 0.0 all-gather.2.cloned.1.call-update
  65.2 0.0 copy-done.2
  65.2 3.2 %collective-permute-start.1 = (bf16[64,25,128]{2,0,1:T(8,128)(2,1)S(1)}, bf16[64,25,128]{2,0,1:T(8,128)(2,1)}, u32[]{:S(2)}, u32[]{:S(2)}) collective-permute-start(bf16[64,25,128]{2,0,1:T(8,128)(2,1)S(1)} %copy-done.2), channel_id=1, source_target_pairs={{1,0},{2,1},{3,2},{4,3},{5,4},{6,5},{7,6},{8,7},{9,8},{10,9},{11,1... | collective-permute-start | bytes 1228808 | tf_op jit(solution)/shard_map/ppermute | solution.py:19
  68.3 0.0 collective-permute-start
  68.3 0.0 copy-done.3
  68.3 0.7 reshape.127.index_ref
  69.0 0.0 copy-done.4
  69.0 0.7 reshape.135.live_ref
  69.7 0.0 copy-done
  69.7 0.4 convert_bitcast_fusion
  70.1 1.8 copy.16
  72.0 2.1 copy.19.frames_ref
  74.1 0.0 copy-start.5
  74.1 1.3 copy.17
  75.5 1.2 copy.20.radial_ref
  76.6 0.0 copy-done.5
  76.6 2.2 %collective-permute-done.1 = bf16[64,25,128]{2,0,1:T(8,128)(2,1)} collective-permute-done((bf16[64,25,128]{2,0,1:T(8,128)(2,1)S(1)}, bf16[64,25,128]{2,0,1:T(8,128)(2,1)}, u32[]{:S(2)}, u32[]{:S(2)}) %collective-permute-start.1) | collective-permute-done | bytes 409632 | tf_op jit(solution)/shard_map/ppermute | solution.py:19
  78.8 9.7 %collective-permute-done = bf16[64,25,128]{2,0,1:T(8,128)(2,1)} collective-permute-done((bf16[64,25,128]{2,0,1:T(8,128)(2,1)S(1)}, bf16[64,25,128]{2,0,1:T(8,128)(2,1)}, u32[]{:S(2)}, u32[]{:S(2)}) %collective-permute-start) | collective-permute-done | bytes 409632 | tf_op jit(solution)/shard_map/ppermute | solution.py:18
  88.5 1.2 pad_maximum_fusion
  89.8 2.3 %copy.18 = bf16[192,25,128]{0,2,1:T(8,128)(2,1)} copy(bf16[192,25,128]{2,0,1:T(8,128)(2,1)S(1)} %pad_maximum_fusion) | data formatting | bytes 2457600 | tf_op jit(solution)/shard_map/concatenate | solution.py:20
  92.0 36.4 %all-gather.2.cloned.1.call-done = bf16[11264,128]{1,0:T(8,128)(2,1)} async-done(((bf16[352,128]{1,0:T(8,128)(2,1)}), bf16[11264,128]{1,0:T(8,128)(2,1)}) %all-gather.2.cloned.1.call-update) | async-done | bytes 2883600 | tf_op jit(solution)/shard_map/all_gather | solution.py:46
  128.5 0.7 broadcast_in_dim.5.scale_ref
  129.1 76.2 %shard_map.109 = f32[64,25,128]{2,1,0:T(8,128)} custom-call(s32[1,3072]{1,0:T(1,128)} %reshape.127.index_ref, f32[1,3072]{1,0:T(1,128)} %reshape.135.live_ref, f32[165,3072]{1,0:T(8,128)} %copy.19.frames_ref, bf16[128,3072]{1,0:T(8,128)(2,1)} %copy.20.radial_ref, bf16[3200,192]{1,0:T(8,128)(2,1)} %bitcast.33, bf16[4,2816,128]{2,1,0:T(8,128)(2,1)} %bitcast.35, ...), custom_call_target="tpu_custom_call" | custom-call | tf_op jit(solution)/shard_map/pallas_call | solution.py:249
  205.4 2.6 %copy.21 = f32[64,25,128]{2,0,1:T(8,128)} copy(f32[64,25,128]{2,1,0:T(8,128)} %shard_map.109) | data formatting | bytes 1638400 | tf_op jit(solution)/shard_map/pallas_call | solution.py:249
  (18 shorter events, 0.2 us)
Async XLA Ops:
  6.5 58.6 %reduce-scatter.2.cloned.1.call-start = ((), (), s32[]{:S(2)}) async-start(), calls=%async_computation.1 | async-start | bytes 811008 | tf_op jit(solution)/shard_map/reduce_scatter | solution.py:45
  11.8 53.3 %copy-start.2 = (bf16[64,25,128]{2,0,1:T(8,128)(2,1)S(1)}, bf16[64,25,128]{2,0,1:T(8,128)(2,1)}, u32[]{:S(2)}) copy-start(bf16[64,25,128]{2,0,1:T(8,128)(2,1)} %param.11) | copy-start | bytes 1228804
  11.8 56.5 %copy-start.3 = (s32[64,48]{0,1:T(8,128)S(1)}, s32[64,48]{0,1:T(8,128)}, u32[]{:S(2)}) copy-start(s32[64,48]{0,1:T(8,128)} %param.14) | copy-start | bytes 36868
  11.9 57.2 %copy-start.4 = (s32[64]{0:T(128)S(1)}, s32[64]{0:T(128)}, u32[]{:S(2)}) copy-start(s32[64]{0:T(128)} %param.15) | copy-start | bytes 772
  11.9 57.8 %copy-start = (bf16[64,48,165]{2,1,0:T(8,128)(2,1)S(1)}, bf16[64,48,165]{2,1,0:T(8,128)(2,1)}, u32[]{:S(2)}) copy-start(bf16[64,48,165]{2,1,0:T(8,128)(2,1)} %param.12) | copy-start | bytes 3041284
  26.6 0.9 copy-start.1
  27.5 101.0 %all-gather.2.cloned.1.call-start = ((), (), s32[]{:S(2)}) async-start(), calls=%async_computation.2 | async-start | bytes 2973696 | tf_op jit(solution)/shard_map/all_gather | solution.py:46
  65.2 13.7 %collective-permute-start.1 = (bf16[64,25,128]{2,0,1:T(8,128)(2,1)S(1)}, bf16[64,25,128]{2,0,1:T(8,128)(2,1)}, u32[]{:S(2)}, u32[]{:S(2)}) collective-permute-start(bf16[64,25,128]{2,0,1:T(8,128)(2,1)S(1)} %copy-done.2), channel_id=1, source_target_pairs={{1,0},{2,1},{3,2},{4,3},{5,4},{6,5},{7,6},{8,7},{9,8},{10,9},{11,1... | collective-permute-start | bytes 1228808 | tf_op jit(solution)/shard_map/ppermute | solution.py:19
  68.3 20.2 %collective-permute-start = (bf16[64,25,128]{2,0,1:T(8,128)(2,1)S(1)}, bf16[64,25,128]{2,0,1:T(8,128)(2,1)}, u32[]{:S(2)}, u32[]{:S(2)}) collective-permute-start(bf16[64,25,128]{2,0,1:T(8,128)(2,1)S(1)} %copy-done.2), channel_id=1, source_target_pairs={{0,1},{1,2},{2,3},{3,4},{4,5},{5,6},{6,7},{7,8},{8,9},{9,10},{10,1... | collective-permute-start | bytes 1228808 | tf_op jit(solution)/shard_map/ppermute | solution.py:18
  74.1 2.5 %copy-start.5 = (s32[64]{0:T(128)S(1)}, s32[64]{0:T(128)}, u32[]{:S(2)}) copy-start(s32[64]{0:T(128)} %param.15) | copy-start | bytes 772
Sparse Core Ops, SparseCore 0:
  27.6 37.4 reduce-scatter.1
  68.0 60.4 all-gather.1

commit v2 on v1

v2 whole, which is shorter than its diff:
```python
import functools

import jax
import jax.numpy as jnp
import numpy as np
from jax import lax
from jax.experimental import pallas as pl
from jax.experimental.pallas import tpu as pltpu
from jax.sharding import PartitionSpec as P

DEGREES = 5
COMPONENTS = DEGREES * DEGREES
AXES = ("wide", "narrow")


def flat_rows(weights):
    return weights.reshape(weights.shape[0], -1, weights.shape[-1])


def exchange_kernel(
    sizes,
    coefficient_ref,
    features_ref,
    *refs,
):
    wide, narrow, count = sizes
    stacks = refs[:count]
    sides_ref, share_ref = refs[count : count + 2]
    staged = refs[count + 2 : 2 * count + 2]
    partial_ref, received_ref, load_sem, halo_send, halo_recv, send_sem, recv_sem = refs[
        2 * count + 2 :
    ]
    my_wide = lax.axis_index("wide")
    my_narrow = lax.axis_index("narrow")
    part = partial_ref.shape[0] // wide

    loads = []
    for at, (stack, stage) in enumerate(zip(stacks, staged)):
        rows = stage.shape[1]
        loads.append(
            pltpu.make_async_copy(
                stack.at[:, pl.ds(pl.multiple_of(my_narrow * rows, 16), rows), :],
                stage,
                load_sem.at[at],
            )
        )
        loads[-1].start()

    total = wide * narrow
    me = my_wide * narrow + my_narrow
    after = lax.rem(me + 1, total)
    before = lax.rem(me + total - 1, total)
    place = lambda flat: (flat // narrow, lax.rem(flat, narrow))
    peers = [(lax.rem(my_wide + hop, wide), my_narrow) for hop in range(1, wide)]
    barrier = pltpu.get_barrier_semaphore()
    for device in [place(after), place(before)] + peers:
        pl.semaphore_signal(
            barrier, inc=1, device_id=device, device_id_type=pl.DeviceIdType.MESH
        )
    pl.semaphore_wait(barrier, wide + 1)

    copies = []
    for side, device in enumerate([place(after), place(before)]):
        copies.append(
            pltpu.make_async_remote_copy(
                src_ref=features_ref,
                dst_ref=sides_ref.at[side],
                send_sem=halo_send.at[side],
                recv_sem=halo_recv.at[side],
                device_id=device,
                device_id_type=pl.DeviceIdType.MESH,
            )
        )

    offset = 0
    for load, stage in zip(loads, staged):
        load.wait()
        experts, rows, columns = stage.shape
        for block in range(columns // 128):
            lanes = pl.ds(block * 128, 128)
            value = coefficient_ref[0] * stage[0, :, lanes].astype(jnp.float32)
            for expert in range(1, experts):
                value = value + coefficient_ref[expert] * stage[expert, :, lanes].astype(
                    jnp.float32
                )
            partial_ref[pl.ds(offset, rows), :] = value.astype(jnp.bfloat16)
            offset += rows
    if offset < partial_ref.shape[0]:
        rest = partial_ref.shape[0] - offset
        partial_ref[pl.ds(offset, rest), :] = jnp.zeros((rest, 128), jnp.bfloat16)

    for hop, device in enumerate(peers):
        target = device[0]
        copies.append(
            pltpu.make_async_remote_copy(
                src_ref=partial_ref.at[pl.ds(pl.multiple_of(target * part, 16), part), :],
                dst_ref=received_ref.at[hop],
                send_sem=send_sem.at[hop],
                recv_sem=recv_sem.at[hop],
                device_id=device,
                device_id_type=pl.DeviceIdType.MESH,
            )
        )
    for copy in copies[2:]:
        copy.start()
    for copy in copies[:2]:
        copy.start()
    for copy in copies[2:]:
        copy.wait()
    summed = partial_ref[pl.ds(pl.multiple_of(my_wide * part, 16), part), :].astype(jnp.float32)
    for hop in range(wide - 1):
        summed = summed + received_ref[hop].astype(jnp.float32)
    share_ref[...] = summed.astype(jnp.bfloat16)
    for copy in copies[:2]:
        copy.wait()


def exchange(features, coefficients, stacks):
    wide = lax.axis_size("wide")
    narrow = lax.axis_size("narrow")
    stacks = [flat_rows(w) for w in stacks]
    staged = [(w.shape[0], w.shape[1] // narrow, w.shape[2]) for w in stacks]
    rows = sum(shape[1] * shape[2] // 128 for shape in staged)
    unit = 16 * wide
    rows = -(-rows // unit) * unit
    anywhere = pl.BlockSpec(memory_space=pl.ANY)
    return pl.pallas_call(
        functools.partial(exchange_kernel, (wide, narrow, len(stacks))),
        in_specs=[pl.BlockSpec(memory_space=pltpu.SMEM)] + [anywhere] * (1 + len(stacks)),
        out_specs=[anywhere, pl.BlockSpec(memory_space=pltpu.VMEM)],
        out_shape=[
            jax.ShapeDtypeStruct((2,) + features.shape, features.dtype),
            jax.ShapeDtypeStruct((rows // wide, 128), jnp.bfloat16),
        ],
        scratch_shapes=[pltpu.VMEM(shape, jnp.bfloat16) for shape in staged]
        + [
            pltpu.VMEM((rows, 128), jnp.bfloat16),
            pltpu.VMEM((wide - 1, rows // wide, 128), jnp.bfloat16),
            pltpu.SemaphoreType.DMA((len(stacks),)),
            pltpu.SemaphoreType.DMA((2,)),
            pltpu.SemaphoreType.DMA((2,)),
            pltpu.SemaphoreType.DMA((wide - 1,)),
            pltpu.SemaphoreType.DMA((wide - 1,)),
        ],
        compiler_params=pltpu.CompilerParams(collective_id=0, has_side_effects=True),
        cost_estimate=pl.CostEstimate(flops=10**9, bytes_accessed=10**7, transcendentals=0),
    )(coefficients, features, *stacks)


def order_starts():
    starts = []
    start = 0
    for order in range(DEGREES):
        starts.append(start)
        start += (DEGREES - order) * (1 if order == 0 else 2)
    return starts


def spread_frames(frames_ref, frame_ref):
    for k in range(frames_ref.shape[0]):
        row = frames_ref[pl.ds(k, 1), :]
        frame_ref[k] = jnp.broadcast_to(row, frame_ref.shape[1:]).astype(jnp.bfloat16)


def rotate_kernel(index_ref, frames_ref, radial_ref, features_ref, turned_ref, source_ref, frame_ref):
    channels, lanes = radial_ref.shape
    extended = features_ref.shape[1]
    spread_frames(frames_ref, frame_ref)

    picked = (
        lax.broadcasted_iota(jnp.int32, (extended, lanes), 0) == index_ref[...]
    ).astype(jnp.bfloat16)
    for component in range(COMPONENTS):
        block = pl.ds(component * channels, channels)
        source_ref[block, :] = jnp.dot(
            features_ref[block, :], picked, preferred_element_type=jnp.float32
        ).astype(jnp.bfloat16)

    starts = order_starts()
    lane_tiles = lanes // 128

    def rotate(i, carried):
        row = pl.multiple_of((i // lane_tiles) * 16, 16)
        lane = pl.ds(pl.multiple_of((i % lane_tiles) * 128, 128), 128)
        tile = lambda place: pl.ds(pl.multiple_of(place * channels + row, 16), 16)
        radial = radial_ref[pl.ds(row, 16), lane]
        offset = 0
        for degree in range(DEGREES):
            size = 2 * degree + 1
            xs = [source_ref[tile(degree * degree + q), lane] for q in range(size)]
            for p in range(size):
                value = frame_ref[offset + p * size, :, lane] * xs[0]
                for q in range(1, size):
                    value = value + frame_ref[offset + p * size + q, :, lane] * xs[q]
                order = abs(p - degree)
                place = starts[order] + degree - order
                if p < degree:
                    place += DEGREES - order
                turned_ref[tile(place), lane] = value * radial
            offset += size * size
        return carried

    lax.fori_loop(0, (channels // 16) * lane_tiles, rotate, 0)


def mix_kernel(
    shapes,
    live_ref,
    frames_ref,
    turned_ref,
    merged_ref,
    scale_ref,
    out_ref,
    gated_ref,
    frame_ref,
    total_ref,
    *weight_refs,
):
    step = pl.program_id(0)
    atoms, _, channels = out_ref.shape
    lanes = live_ref.shape[1]
    members = merged_ref.shape[0]
    lane_tiles = lanes // 128
    starts = order_starts()

    @pl.when(step == 0)
    def _():
        total_ref[...] = jnp.zeros_like(total_ref)
        offset = 0
        for weight_ref, (rows, columns) in zip(weight_refs, shapes):
            part = rows // members
            for block in range(columns // 128):
                whole = jnp.concatenate(
                    [merged_ref[m, pl.ds(offset, part), :] for m in range(members)], axis=0
                )
                weight_ref[pl.ds(block * 128, 128), :] = jnp.transpose(whole)
                offset += part

    spread_frames(frames_ref, frame_ref)

    central = jnp.dot(
        weight_refs[0][...],
        turned_ref[pl.ds(0, DEGREES * channels), :],
        preferred_element_type=jnp.float32,
    )
    scalar = central[:channels]
    gate = live_ref[...] / (1.0 + jnp.exp(-scalar))
    for degree in range(DEGREES):
        gated_ref[pl.ds((degree * degree + degree) * channels, channels), :] = (
            central[degree * channels : (degree + 1) * channels] * gate
        ).astype(jnp.bfloat16)
    for order in range(1, DEGREES):
        kept = DEGREES - order
        height = kept * channels
        plus = turned_ref[pl.ds(starts[order] * channels, height), :]
        minus = turned_ref[pl.ds(starts[order] * channels + height, height), :]
        for side in range(2):
            pair = [plus, -minus] if side == 0 else [minus, plus]
            mixed = jnp.dot(
                weight_refs[order][...],
                jnp.concatenate(pair, axis=0),
                preferred_element_type=jnp.float32,
            )
            for column in range(kept):
                degree = order + column
                component = degree * degree + degree + (order if side == 0 else -order)
                gated_ref[pl.ds(component * channels, channels), :] = (
                    mixed[column * channels : (column + 1) * channels] * gate
                ).astype(jnp.bfloat16)

    def unrotate(i, carried):
        row = pl.multiple_of(i * 16, 16)
        offset = 0
        for degree in range(DEGREES):
            size = 2 * degree + 1
            sums = [None] * size
            for tile in range(lane_tiles):
                lane = pl.ds(tile * 128, 128)
                ys = [
                    gated_ref[
                        pl.ds(pl.multiple_of((degree * degree + q) * channels + row, 16), 16), lane
                    ]
                    for q in range(size)
                ]
                for p in range(size):
                    value = frame_ref[offset + p, :, lane] * ys[0]
                    for q in range(1, size):
                        value = value + frame_ref[offset + q * size + p, :, lane] * ys[q]
                    value = value.astype(jnp.float32)
                    sums[p] = value if sums[p] is None else sums[p] + value
            for p in range(size):
                place = pl.ds(pl.multiple_of((degree * degree + p) * channels + row, 16), 16)
                total_ref[place, :] = total_ref[place, :] + sums[p]
            offset += size * size
        return carried

    lax.fori_loop(0, channels // 16, unrotate, 0)

    @pl.when(step == pl.num_programs(0) - 1)
    def _():
        for component in range(COMPONENTS):
            block = jnp.transpose(total_ref[pl.ds(component * channels, channels), :])
            total = block[:atoms]
            for part in range(1, 128 // atoms):
                total = total + block[part * atoms : (part + 1) * atoms]
            out_ref[:, component, :] = total * scale_ref[...]


def body(
    node_features,
    frames,
    radial,
    neighbours,
    counts,
    coefficients,
    w_zero,
    w_one,
    w_two,
    w_three,
    w_four,
):
    atoms, components, channels = node_features.shape
    slots = neighbours.shape[1]
    entries = frames.shape[2]
    edges = atoms * slots
    stacks = (w_zero, w_one, w_two, w_three, w_four)
    sides, share = exchange(node_features, coefficients, stacks)
    merged = lax.all_gather(share, ("narrow", "wide"), axis=0, tiled=True)
    merged = merged.reshape(lax.axis_size("narrow"), -1, 128)
    shapes = [(int(np.prod(w.shape[1:-1])), w.shape[-1]) for w in stacks]

    features = jnp.concatenate([sides[0], node_features, sides[1]], axis=0)
    features = features.reshape(3 * atoms, components * channels).T
    block_start = lax.axis_index(AXES) * atoms
    atoms_total = atoms * lax.axis_size(AXES)
    index = ((neighbours - block_start + atoms) % atoms_total).T.reshape(1, edges)
    live = (lax.broadcasted_iota(jnp.int32, (slots, atoms), 0) < counts[None, :]).astype(
        jnp.float32
    ).reshape(1, edges)
    frames_t = frames.transpose(2, 1, 0).reshape(entries, edges).astype(jnp.float32)
    radial_t = radial.transpose(2, 1, 0).reshape(channels, edges)
    scale = jnp.broadcast_to(
        (1.0 / jnp.sqrt(counts.astype(jnp.float32)))[:, None], (atoms, channels)
    )

    lanes = 256
    whole = lambda shape: pl.BlockSpec(shape, lambda i: (0,) * len(shape))
    columns = lambda rows: pl.BlockSpec((rows, lanes), lambda i: (0, i))
    params = pltpu.CompilerParams(
        dimension_semantics=("arbitrary",), vmem_limit_bytes=56 * 1024 * 1024
    )
    turned = pl.pallas_call(
        rotate_kernel,
        grid=(edges // lanes,),
        in_specs=[columns(1), columns(entries), columns(channels), whole(features.shape)],
        out_specs=columns(components * channels),
        out_shape=jax.ShapeDtypeStruct((components * channels, edges), jnp.bfloat16),
        scratch_shapes=[
            pltpu.VMEM((components * channels, lanes), jnp.bfloat16),
            pltpu.VMEM((entries, 16, lanes), jnp.bfloat16),
        ],
        compiler_params=params,
        cost_estimate=pl.CostEstimate(
            flops=2 * 3 * atoms * components * channels * edges,
            bytes_accessed=2 * components * channels * edges,
            transcendentals=0,
        ),
    )(index, frames_t, radial_t, features)
    return pl.pallas_call(
        functools.partial(mix_kernel, shapes),
        grid=(edges // lanes,),
        in_specs=[
            columns(1),
            columns(entries),
            columns(components * channels),
            whole(merged.shape),
            whole(scale.shape),
        ],
        out_specs=whole((atoms, components, channels)),
        out_shape=jax.ShapeDtypeStruct((atoms, components, channels), jnp.float32),
        scratch_shapes=[
            pltpu.VMEM((components * channels, lanes), jnp.bfloat16),
            pltpu.VMEM((entries, 16, lanes), jnp.bfloat16),
            pltpu.VMEM((components * channels, 128), jnp.float32),
        ]
        + [pltpu.VMEM((n, k), jnp.bfloat16) for k, n in shapes],
        compiler_params=params,
    )(live, frames_t, turned, merged, scale)


def solution(mesh):
    spread = lambda rest: P(AXES, *([None] * rest))
    in_specs = (
        spread(2),
        spread(2),
        spread(2),
        spread(1),
        spread(0),
        P("wide"),
        P("wide", None, None),
        P("wide", None, None, None),
        P("wide", None, None, None),
        P("wide", None, None, None),
        P("wide", None, None, None),
    )
    return jax.shard_map(body, mesh=mesh, in_specs=in_specs, out_specs=spread(2), check_vma=False)
```

time: 215 us -> 156 us (0.73)
  waiting for transfers between devices: 86 us -> 10.1 us
  Pallas kernels: 76.2 us -> 111 us
  other arithmetic: 20 us -> 2.51 us
  starting transfers between devices: 3.2 us -> 0.01 us
  local copies, waits for them, and re-layouts: 15.9 us -> 18.8 us
    reduce_scatter x1 -> x0, waiting for transfers between devices: 37.6 us -> none  [merge_weights(): share = lax.psum_scatter(partial, 'wide', scatter_dimension=0, tiled=True)]
    pallas_call x1 -> x3, Pallas kernels: 76.2 us -> 111 us  [the longest x1 45.7 us: body(): pl.pallas_call(functools.partial(mix_kernel, shapes), grid=(edges // lane...]
    all_gather x1, waiting for transfers between devices: 36.4 us -> 10.1 us  [body(): merged = lax.all_gather(share, ('narrow', 'wide'), axis=0, tiled=True)]
    convert_element_type x4 -> x0, other arithmetic: 15 us -> none  [merge_weights(): total = total.astype(jnp.bfloat16)]
    ppermute x2 -> x0, waiting for transfers between devices: 11.9 us -> none  [the longest x1 9.7 us: halo(): lax.ppermute(cells, AXES, [(i, (i + 1) % count) for i in range(count)])]
    unnamed x1 -> x0, other arithmetic: 3.27 us -> none
    ppermute x2 -> x0, starting transfers between devices: 3.16 us -> none  [the longest x1 3.15 us: halo(): lax.ppermute(cells, AXES, [((i + 1) % count, i) for i in range(count)])]
    slice x1 -> x3, local copies, waits for them, and re-layouts: 1.42 us -> 4.19 us  [body(): features = jnp.concatenate([sides[0], node_features, sides[1]], axis=0)]
  transfers between devices with their start and end apart: 4 -> 1, of which waited for: 4 -> 1; matrix products, arithmetic and copies ran while one was open for 5% -> 10% of each run, Pallas kernels for 0% -> 21%
where the time goes in v2:
time: 156 us
  Pallas kernels  111 us (71%)
  local copies, waits for them, and re-layouts  18.8 us (12%)
  between operations  13.5 us (9%)
  waiting for transfers between devices  10.1 us (6%)
  other arithmetic  2.51 us (2%)
    pallas_call x1, Pallas kernels, body(): pl.pallas_call(functools.partial(mix_kernel, shapes), grid=(edges // lane...  45.7 us
    pallas_call x1, Pallas kernels, body(): pl.pallas_call(rotate_kernel, grid=(edges // lanes,), in_specs=[columns(1...  33.3 us
    pallas_call x1, Pallas kernels, exchange(): pl.pallas_call(functools.partial(exchange_kernel, (wide, narrow, len(stac...  31.6 us
    all_gather x1, waiting for transfers between devices, body(): merged = lax.all_gather(share, ('narrow', 'wide'), axis=0, tiled=True)  10.1 us
    unnamed x17, local copies, waits for them, and re-layouts  4.86 us
    slice x3, local copies, waits for them, and re-layouts, body(): features = jnp.concatenate([sides[0], node_features, sides[1]], axis=0)  4.19 us
    convert_element_type x2, local copies, waits for them, and re-layouts, body(): frames.transpose(2, 1, 0).reshape(entries, edges).astype(jnp.float32)  3.94 us
  transfers between devices with their start and end apart: 1, of which 1 were waited for; matrix products, arithmetic and copies ran while one was open for 10% of the time, Pallas kernels for 21%

profile of v2, /device:TPU:0, one launch (start us, length us, event | category | flops | bytes accessed | tf_op | source)
XLA Modules:
  0.0 155.6 jit_solution(11901798832091616153)
XLA Ops:
  6.5 0.0 all-gather.2.cloned.1.call-start
  6.5 2.1 %copy.21.features_ref = bf16[64,25,128]{2,1,0:T(8,128)(2,1)} copy(bf16[64,25,128]{2,0,1:T(8,128)(2,1)} %param.11) | data formatting | bytes 819200 | tf_op args[0]
  8.6 0.0 copy-start.3
  8.6 31.6 %shard_map.109 = (bf16[2,64,25,128]{3,2,1,0:T(8,128)(2,1)}, bf16[352,128]{1,0:T(8,128)(2,1)}) custom-call(f32[4]{0:T(128)} %coefficient_ref.1, bf16[64,25,128]{2,1,0:T(8,128)(2,1)} %copy.21.features_ref, bf16[4,640,640]{2,1,0:T(8,128)(2,1)} %refs_0_.1, bf16[4,1024,512]{2,1,0:T(8,128)(2,1)} %bitcast.19, bf16[4,768,384]{2,1,0:T(8,128)(2,1)} %bitcast.25, ...), custom_call_target="tpu_custom_call" | custom-call | flops 1000000000 | bytes 10000000 | tf_op jit(solution)/shard_map/pallas_call | solution.py:127
  40.2 0.0 copy-start.5
  40.2 0.0 copy-start.4
  40.2 0.0 all-gather.2.cloned.1.call-update
  40.3 0.0 copy-done.3
  40.3 1.3 copy.23
  41.5 1.3 fusion.3
  42.8 1.5 copy.24
  44.3 1.5 copy.22
  45.7 0.0 copy-done.5
  45.7 0.7 reshape.60.index_ref
  46.4 0.0 copy-done.4
  46.4 0.4 convert_bitcast_fusion
  46.8 1.8 %copy.19 = f32[165,48,64]{0,2,1:T(8,128)S(1)} copy(f32[165,48,64]{0,1,2:T(8,128)S(1)} %convert_bitcast_fusion) | data formatting | bytes 4055040 | tf_op jit(solution)/shard_map/convert_element_type | solution.py:340
  48.7 0.0 copy-start.6
  48.7 2.1 %copy.27.frames_ref = f32[165,3072]{1,0:T(8,128)} copy(f32[165,3072]{0,1:T(8,128)S(1)} %bitcast.18) | data formatting | bytes 4055040 | tf_op jit(solution)/shard_map/convert_element_type | solution.py:340
  50.8 0.0 copy-start
  50.8 0.0 copy-start.1
  50.8 0.0 copy-start.2
  50.8 1.5 copy.20
  52.3 1.2 copy.26.radial_ref
  53.5 0.0 copy-done.6
  53.5 0.7 reshape.67.live_ref
  54.2 0.0 copy-done
  54.2 0.0 copy-done.1
  54.2 0.0 copy-done.2
  54.2 2.1 %maximum_bitcast_fusion.features_ref = bf16[3200,192]{1,0:T(8,128)(2,1)} fusion(bf16[64,3200]{0,1:T(8,128)(2,1)S(1)} %bitcast.21, bf16[64,3200]{0,1:T(8,128)(2,1)S(1)} %bitcast.20, bf16[64,3200]{0,1:T(8,128)(2,1)S(1)} %bitcast.22), kind=kLoop, calls=%fused_computation.1 | loop fusion | flops 3686400 | bytes 2457600 | tf_op jit(solution)/shard_map/transpose | solution.py:333
  56.2 33.3 %shard_map.110.turned_ref = bf16[3200,3072]{1,0:T(8,128)(2,1)} custom-call(s32[1,3072]{1,0:T(1,128)} %reshape.60.index_ref, f32[165,3072]{1,0:T(8,128)} %copy.27.frames_ref, bf16[128,3072]{1,0:T(8,128)(2,1)} %copy.26.radial_ref, bf16[3200,192]{1,0:T(8,128)(2,1)} %maximum_bitcast_fusion.features_ref), custom_call_target="tpu_custom_call" | custom-call | flops 3774873600 | bytes 19660800 | tf_op jit(solution)/shard_map/pallas_call | solution.py:352
  89.6 10.1 %all-gather.2.cloned.1.call-done = bf16[11264,128]{1,0:T(8,128)(2,1)} async-done(((bf16[352,128]{1,0:T(8,128)(2,1)}), bf16[11264,128]{1,0:T(8,128)(2,1)}) %all-gather.2.cloned.1.call-update) | async-done | bytes 2883600 | tf_op jit(solution)/shard_map/all_gather | solution.py:328
  99.7 0.7 broadcast_in_dim.2.scale_ref
  100.4 45.7 %shard_map.111 = f32[64,25,128]{2,1,0:T(8,128)} custom-call(f32[1,3072]{1,0:T(1,128)} %reshape.67.live_ref, f32[165,3072]{1,0:T(8,128)} %copy.27.frames_ref, bf16[3200,3072]{1,0:T(8,128)(2,1)} %shard_map.110.turned_ref, bf16[4,2816,128]{2,1,0:T(8,128)(2,1)} %bitcast.24, f32[64,128]{1,0:T(8,128)} %broadcast_in_dim.2.scale_ref), custom_call_target="tpu_custom_call" | custom-call | tf_op jit(solution)/shard_map/pallas_call | solution.py:369
  146.1 2.6 %copy.28 = f32[64,25,128]{2,0,1:T(8,128)} copy(f32[64,25,128]{2,1,0:T(8,128)} %shard_map.111) | data formatting | bytes 1638400 | tf_op jit(solution)/shard_map/pallas_call | solution.py:369
  (3 shorter events, 0.0 us)
Async XLA Ops:
  6.5 93.2 %all-gather.2.cloned.1.call-start = ((), (), s32[]{:S(2)}) async-start(), calls=%async_computation | async-start | bytes 2973696 | tf_op jit(solution)/shard_map/all_gather | solution.py:328
  8.6 31.6 %copy-start.3 = (bf16[64,25,128]{2,0,1:T(8,128)(2,1)S(1)}, bf16[64,25,128]{2,0,1:T(8,128)(2,1)}, u32[]{:S(2)}) copy-start(bf16[64,25,128]{2,0,1:T(8,128)(2,1)} %param.11) | copy-start | bytes 1228804
  40.2 5.5 %copy-start.5 = (s32[64,48]{0,1:T(8,128)S(1)}, s32[64,48]{0,1:T(8,128)}, u32[]{:S(2)}) copy-start(s32[64,48]{0,1:T(8,128)} %param.14) | copy-start | bytes 36868
  40.2 6.2 %copy-start.4 = (bf16[64,48,165]{2,1,0:T(8,128)(2,1)S(1)}, bf16[64,48,165]{2,1,0:T(8,128)(2,1)}, u32[]{:S(2)}) copy-start(bf16[64,48,165]{2,1,0:T(8,128)(2,1)} %param.12) | copy-start | bytes 3041284
  48.7 4.8 %copy-start.6 = (s32[64]{0:T(128)S(1)}, s32[64]{0:T(128)}, u32[]{:S(2)}) copy-start(s32[64]{0:T(128)} %param.15) | copy-start | bytes 772
  50.8 3.4 %copy-start = (bf16[64,25,128]{0,2,1:T(8,128)(2,1)S(1)}, bf16[64,25,128]{0,2,1:T(8,128)(2,1)}, u32[]{:S(2)}) copy-start(bf16[64,25,128]{0,2,1:T(8,128)(2,1)} %copy.23) | copy-start | bytes 1228804
  50.8 3.4 %copy-start.1 = (bf16[1,64,25,128]{1,3,2,0:T(8,128)(2,1)S(1)}, bf16[1,64,25,128]{1,3,2,0:T(8,128)(2,1)}, u32[]{:S(2)}) copy-start(bf16[1,64,25,128]{1,3,2,0:T(8,128)(2,1)} %copy.24) | copy-start | bytes 1228804
  50.8 3.4 %copy-start.2 = (bf16[1,64,25,128]{1,3,2,0:T(8,128)(2,1)S(1)}, bf16[1,64,25,128]{1,3,2,0:T(8,128)(2,1)}, u32[]{:S(2)}) copy-start(bf16[1,64,25,128]{1,3,2,0:T(8,128)(2,1)} %copy.22) | copy-start | bytes 1228804
Sparse Core Ops, SparseCore 0:
  40.4 59.2 all-gather.1
